TPU v7x, 32 devices: a whole 2x2x4 slice. The times are simulated.
32 devices in a mesh: rep: 1, r: 8 (over y, z), s: 4 (over x, core).
Axes of the slice: x: 2, y: 2, z: 4, core: 2. Of those that a mesh axis runs over, the one named last changes fastest.
Arguments:
- x: bfloat16 [32, 4096, 640], P(('rep', 'r', 's'))
- dy: bfloat16 [32, 4096, 640], P(('rep', 'r', 's'))
- w_gate: bfloat16 [2, 640, 2176], P(None, 's')
- w_up: bfloat16 [2, 640, 2176], P(None, 's')
- w_down: bfloat16 [2, 2176, 640], P(None, 's')
Outputs:
- output 1: bfloat16 [32, 4096, 640], P(('rep', 'r', 's'))
- output 2: bfloat16 [2, 640, 2176], P('rep', 's')
- output 3: bfloat16 [2, 640, 2176], P('rep', 's')
- output 4: bfloat16 [2, 2176, 640], P('rep', 's')
All inputs are finite; a program needn't handle non-finite values.
Results may differ from a plain program's by a relative error of at most 0.018.
Values are sent between devices in bfloat16 or wider.
A program may use at most 2 GiB of HBM per device.

v0:
```python
import jax
import jax.numpy as jnp
from jax import lax
from jax.sharding import PartitionSpec as P

NAMES = ("w_gate", "w_up", "w_down")


def matmul(a, w):
    return jnp.dot(a, w, preferred_element_type=jnp.float32).astype(jnp.bfloat16)


def normed(h):
    wide = h.astype(jnp.float32)
    scale = lax.rsqrt(jnp.mean(wide**2, -1, keepdims=True) + 1e-6)
    return (wide * scale).astype(jnp.bfloat16)


def layer(h, w):
    a = normed(h)
    gate = jnp.dot(a, w["w_gate"], preferred_element_type=jnp.float32)
    up = jnp.dot(a, w["w_up"], preferred_element_type=jnp.float32)
    return h + matmul((jax.nn.silu(gate) * up).astype(jnp.bfloat16), w["w_down"])


def solution(mesh):
    def fetched(weights, number):
        return {name: lax.all_gather(w[number], "s", axis=0, tiled=True) for name, w in zip(NAMES, weights, strict=True)}

    def summed(term):
        return lax.psum(lax.psum_scatter(term, "s", scatter_dimension=0, tiled=True), "r")

    def step(x, dy, *weights):
        layers = weights[0].shape[0]
        h, inputs = x[0], []
        for number in range(layers):
            inputs.append(h)
            h = layer(h, fetched(weights, number))
        by_h, mine = dy[0], [None] * layers
        for number in reversed(range(layers)):
            _, back = jax.vjp(lambda w, h: layer(h, w), fetched(weights, number), inputs[number])
            by_w, by_h = back(by_h)
            mine[number] = [summed(by_w[name]) for name in NAMES]
        return (by_h[None], *(jnp.stack([mine[number][i] for number in range(layers)]) for i in range(3)))

    states, cut = P(("rep", "r", "s"), None, None), P(None, "s", None)
    return jax.shard_map(
        step,
        mesh=mesh,
        in_specs=(states, states) + (cut,) * 3,
        out_specs=(states,) + (P("rep", "s", None),) * 3,
        check_vma=False,
    )
```

profile of v0, /device:TPU:0, one launch (start us, length us, event | category | flops | bytes accessed | tf_op | source)
XLA Modules:
  0.0 726.9 jit_solution(11342129456093164731)
XLA Ops:
  16.7 7.9 %copy.10 = bf16[1,4096,640]{1,2,0:T(8,128)(2,1)} copy(bf16[1,4096,640]{2,1,0:T(8,128)(2,1)} %param.5) | data formatting | bytes 10485760 | tf_op args[0]
  28.8 8.0 %copy.9 = bf16[1,4096,640]{1,2,0:T(8,128)(2,1)} copy(bf16[1,4096,640]{2,1,0:T(8,128)(2,1)} %param.6) | data formatting | bytes 10485760 | tf_op args[1]
  39.0 23.6 %fusion.45 = f32[4096,2176]{1,0:T(8,128)} fusion(bf16[1,4096,640]{1,2,0:T(8,128)(2,1)} %copy.10, f32[4096]{0:T(1024)S(1)} %fusion.58, bf16[1,640,2176]{2,1,0:T(8,128)(2,1)} %all-gather.13.cloned.1.call-done), kind=kOutput, calls=%fused_computation.65 | convolution fusion | flops 11416371200 | bytes 43696128 | tf_op jit(solution)/shard_map/dot_general | solution.py:21
  66.8 36.1 %multiply_convert_fusion.1 = (bf16[4096,2176]{1,0:T(8,128)(2,1)}, f32[4096,2176]{1,0:T(8,128)}) fusion(f32[4096,2176]{1,0:T(8,128)} %fusion.45, bf16[1,640,2176]{2,1,0:T(8,128)(2,1)} %all-gather.15.cloned.1.call-done, bf16[1,4096,640]{1,2,0:T(8,128)(2,1)} %copy.10, f32[4096]{0:T(1024)S(1)} %fusion.58), kind=kOutput, calls=%fused_computation.13 | convolution fusion | flops 11469848576 | bytes 97173504 | tf_op jit(solution)/shard_map/dot_general | solution.py:22
  102.9 20.0 %fusion.18 = (f32[4096]{0:T(1024)S(1)}, bf16[4096,640]{0,1:T(8,128)(2,1)}) fusion(bf16[4096,2176]{1,0:T(8,128)(2,1)} %get-tuple-element.20, bf16[1,2176,640]{2,1,0:T(8,128)(2,1)} %all-gather.17.cloned.1.call-done, bf16[1,4096,640]{1,2,0:T(8,128)(2,1)} %copy.10), kind=kOutput, calls=%fused_computation.40 | convolution fusion | flops 11421609984 | bytes 31113216 | tf_op jit(solution)/shard_map/dot_general | solution.py:10
  122.9 21.1 %convolution_convert_fusion.1 = bf16[4096,2176]{1,0:T(8,128)(2,1)} fusion(bf16[1,4096,640]{2,1,0:T(8,128)(2,1)} %param.6, bf16[1,2176,640]{2,1,0:T(8,128)(2,1)} %all-gather.21.cloned.1.call-done), kind=kOutput, calls=%fused_computation.21 | convolution fusion | flops 11417419776 | bytes 25853952 | tf_op jit(solution)/shard_map/transpose(jvp())/dot_general | solution.py:10
  150.3 24.0 %fusion.37 = f32[4096,2176]{1,0:T(8,128)} fusion(bf16[4096,640]{0,1:T(8,128)(2,1)} %get-tuple-element.23, f32[4096]{0:T(1024)S(1)} %fusion.59, bf16[1,640,2176]{2,1,0:T(8,128)(2,1)} %all-gather.23.cloned.1.call-done), kind=kOutput, calls=%fused_computation.62 | convolution fusion | flops 11416371200 | bytes 43696128 | tf_op jit(solution)/shard_map/jvp()/dot_general | solution.py:22
  178.5 47.6 %fusion.1 = (bf16[4096,2176]{1,0:T(8,128)(2,1)}, f32[4096,2176]{1,0:T(8,128)}) fusion(f32[4096,2176]{1,0:T(8,128)} %fusion.37, bf16[4096,2176]{1,0:T(8,128)(2,1)} %convolution_convert_fusion.1, bf16[1,640,2176]{2,1,0:T(8,128)(2,1)} %all-gather.19.cloned.1.call-done, bf16[4096,640]{0,1:T(8,128)(2,1)} %get-tuple-element.23, f32[4096]{0:T(1024)S(1)} %fusion.59), kind=kOutput, calls=%fused_computation.7 | convolution fusion | flops 11523325952 | bytes 114999296 | tf_op jit(solution)/shard_map/jvp()/dot_general | solution.py:21
  226.0 18.5 %convolution_convert_fusion.3 = bf16[4096,640]{0,1:T(8,128)(2,1)} fusion(bf16[4096,2176]{1,0:T(8,128)(2,1)} %get-tuple-element.24, bf16[1,640,2176]{2,1,0:T(8,128)(2,1)} %all-gather.19.cloned.1.call-done), kind=kOutput, calls=%fused_computation.46 | convolution fusion | flops 11408506880 | bytes 25853952 | tf_op jit(solution)/shard_map/transpose(jvp())/dot_general | solution.py:21
  244.6 26.7 %fusion.20 = (f32[4096]{0:T(1024)S(1)}, bf16[4096,640]{0,1:T(8,128)(2,1)}) fusion(bf16[4096,640]{0,1:T(8,128)(2,1)} %get-tuple-element.23, bf16[4096,640]{0,1:T(8,128)(2,1)} %convolution_convert_fusion.3, bf16[1,640,2176]{2,1,0:T(8,128)(2,1)S(1)} %copy-done.10, bf16[4096,2176]{1,0:T(8,128)(2,1)} %convolution_convert_fusion.1, ...), kind=kOutput, calls=%fused_computation.42 | convolution fusion | flops 11477708800 | bytes 72007680 | tf_op jit(solution)/shard_map/transpose(jvp())/dot_general | solution.py:22
  271.3 11.9 %fusion.25 = bf16[4096,640]{0,1:T(8,128)(2,1)} fusion(bf16[4096,640]{0,1:T(8,128)(2,1)} %get-tuple-element.23, bf16[4096,640]{0,1:T(8,128)(2,1)} %get-tuple-element.27, bf16[1,4096,640]{1,2,0:T(8,128)(2,1)} %copy.9, f32[4096]{0:T(1024)S(1)} %multiply_multiply_fusion.1, f32[4096]{0:T(1024)S(1)} %fusion.59), kind=kLoop, calls=%fused_computation.50 | loop fusion | flops 18350080 | bytes 21004288 | tf_op jit(solution)/shard_map/transpose(jvp())/add_any | solution.py:14
  283.3 20.9 %convolution_convert_fusion.5 = bf16[2176,640]{1,0:T(8,128)(2,1)} fusion(bf16[4096,2176]{1,0:T(8,128)(2,1)} %get-tuple-element.20, bf16[4096,640]{0,1:T(8,128)(2,1)} %fusion.25), kind=kOutput, calls=%fused_computation.58 | convolution fusion | flops 11409899520 | bytes 25853952 | tf_op jit(solution)/shard_map/transpose(jvp())/dot_general | solution.py:10
  304.3 29.4 %fusion.32 = bf16[2176,640]{1,0:T(8,128)(2,1)} fusion(bf16[1,4096,640]{2,1,0:T(8,128)(2,1)} %param.6, f32[4096,2176]{1,0:T(8,128)} %fusion.37, f32[4096,2176]{1,0:T(8,128)} %get-tuple-element.25), kind=kOutput, calls=%fused_computation.59 | convolution fusion | flops 11463376896 | bytes 79331328 | tf_op jit(solution)/shard_map/transpose(jvp())/dot_general | solution.py:10
  333.8 46.8 %fusion.3 = (bf16[4096,2176]{1,0:T(8,128)(2,1)}, bf16[4096,2176]{1,0:T(8,128)(2,1)}) fusion(f32[4096,2176]{1,0:T(8,128)} %fusion.45, f32[4096,2176]{1,0:T(8,128)} %get-tuple-element.21, bf16[4096,640]{0,1:T(8,128)(2,1)} %fusion.25, bf16[1,2176,640]{2,1,0:T(8,128)(2,1)S(1)} %copy-done.9), kind=kOutput, calls=%fused_computation.9 | convolution fusion | flops 11524374528 | bytes 114982912 | tf_op jit(solution)/shard_map/transpose(jvp())/dot_general | solution.py:10
  380.6 25.1 %fusion.30 = bf16[640,2176]{1,0:T(8,128)(2,1)} fusion(bf16[4096,2176]{1,0:T(8,128)(2,1)} %get-tuple-element.29, bf16[1,4096,640]{1,2,0:T(8,128)(2,1)} %copy.10, f32[4096]{0:T(1024)S(1)} %copy-done.3, f32[4096,2176]{1,0:T(8,128)} %fusion.45), kind=kOutput, calls=%fused_computation.56 | convolution fusion | flops 11471241216 | bytes 61521920 | tf_op jit(solution)/shard_map/transpose(jvp())/dot_general | solution.py:22
  405.8 25.1 %fusion.31 = bf16[640,2176]{1,0:T(8,128)(2,1)} fusion(bf16[4096,2176]{1,0:T(8,128)(2,1)} %convolution_convert_fusion.1, bf16[4096,640]{0,1:T(8,128)(2,1)} %get-tuple-element.23, f32[4096]{0:T(1024)S(1)} %copy-done.5, f32[4096,2176]{1,0:T(8,128)} %get-tuple-element.25), kind=kOutput, calls=%fused_computation.57 | convolution fusion | flops 11471241216 | bytes 61521920 | tf_op jit(solution)/shard_map/transpose(jvp())/dot_general | solution.py:22
  431.0 18.0 %convolution_convert_fusion.6 = bf16[640,2176]{1,0:T(8,128)(2,1)} fusion(bf16[4096,2176]{1,0:T(8,128)(2,1)} %get-tuple-element.24, bf16[4096,640]{0,1:T(8,128)(2,1)} %get-tuple-element.23, f32[4096]{0:T(1024)S(1)} %copy-done.5), kind=kOutput, calls=%fused_computation.60 | convolution fusion | flops 11416371200 | bytes 25870336 | tf_op jit(solution)/shard_map/transpose(jvp())/dot_general | solution.py:21
  449.1 18.0 %convolution_convert_fusion.7 = bf16[640,2176]{1,0:T(8,128)(2,1)} fusion(bf16[4096,2176]{1,0:T(8,128)(2,1)} %get-tuple-element.28, bf16[1,4096,640]{1,2,0:T(8,128)(2,1)} %copy.10, f32[4096]{0:T(1024)S(1)} %copy-done.3), kind=kOutput, calls=%fused_computation.61 | convolution fusion | flops 11416371200 | bytes 25870336 | tf_op jit(solution)/shard_map/transpose(jvp())/dot_general | solution.py:21
  467.2 18.8 %convolution_convert_fusion.2 = bf16[4096,640]{0,1:T(8,128)(2,1)} fusion(bf16[4096,2176]{1,0:T(8,128)(2,1)} %get-tuple-element.28, bf16[1,640,2176]{2,1,0:T(8,128)(2,1)} %all-gather.13.cloned.1.call-done), kind=kOutput, calls=%fused_computation.45 | convolution fusion | flops 11408506880 | bytes 25853952 | tf_op jit(solution)/shard_map/transpose(jvp())/dot_general | solution.py:21
  486.1 30.6 %reduce-scatter.9.cloned.1.call-done = bf16[160,2176]{1,0:T(8,128)(2,1)} async-done(((bf16[640,2176]{1,0:T(8,128)(2,1)}), bf16[160,2176]{1,0:T(8,128)(2,1)}) %reduce-scatter.9.cloned.1.call-update) | async-done | bytes 696336 | tf_op jit(solution)/shard_map/reduce_scatter | solution.py:31
  516.7 37.7 %reduce-scatter.7.cloned.1.call-done = bf16[160,2176]{1,0:T(8,128)(2,1)} async-done(((bf16[640,2176]{1,0:T(8,128)(2,1)}), bf16[160,2176]{1,0:T(8,128)(2,1)}) %reduce-scatter.7.cloned.1.call-update) | async-done | bytes 696336 | tf_op jit(solution)/shard_map/reduce_scatter | solution.py:31
  554.5 27.0 %fusion.17 = (f32[4096]{0:T(1024)S(1)}, bf16[4096,640]{0,1:T(8,128)(2,1)}) fusion(bf16[1,4096,640]{1,2,0:T(8,128)(2,1)} %copy.10, bf16[4096,640]{0,1:T(8,128)(2,1)} %convolution_convert_fusion.2, bf16[1,640,2176]{2,1,0:T(8,128)(2,1)S(1)} %copy-done.8, bf16[4096,2176]{1,0:T(8,128)(2,1)} %get-tuple-element.29, f32[4096,2176]{1,0:T(8,128)} %fusion.45), kind=kOutput, calls=%fused_computation.39 | convolution fusion | flops 11477708800 | bytes 72007680 | tf_op jit(solution)/shard_map/transpose(jvp())/dot_general | solution.py:22
  581.5 11.9 %fusion.24 = bf16[1,4096,640]{1,2,0:T(8,128)(2,1)} fusion(bf16[4096,640]{0,1:T(8,128)(2,1)} %fusion.25, bf16[4096,640]{0,1:T(8,128)(2,1)} %get-tuple-element.31, bf16[1,4096,640]{1,2,0:T(8,128)(2,1)} %copy.10, f32[4096]{0:T(1024)S(1)} %multiply_multiply_fusion, f32[4096]{0:T(1024)S(1)} %copy-done.3), kind=kLoop, calls=%fused_computation.49 | loop fusion | flops 18350080 | bytes 21004288 | tf_op jit(solution)/shard_map/broadcast_in_dim | solution.py:44
  601.2 112.5 %all-reduce.3.cloned.1.call-done = (bf16[1,160,2176]{2,1,0:T(8,128)(2,1)}, bf16[1,160,2176]{2,1,0:T(8,128)(2,1)}, bf16[1,160,2176]{2,1,0:T(8,128)(2,1)}, bf16[1,...) async-done(((bf16[1,160,2176]{2,1,0:T(8,128)(2,1)}, bf16[1,160,2176]{2,1,0:T(8,128)(2,1)}, bf16[1,160,2176]{2,1,0:T(8,128)(2,1)}, ...) | async-done | bytes 4177936 | tf_op jit(solution)/shard_map/psum | solution.py:31
  (69 shorter events, 44.9 us)
Async XLA Ops:
  7.2 31.9 %all-gather.13.cloned.1.call-start = ((), (), s32[]{:S(2)}) async-start(), calls=%async_computation.12 | async-start | bytes 3481600 | tf_op jit(solution)/shard_map/all_gather | solution.py:28
  9.7 57.1 %all-gather.15.cloned.1.call-start = ((), (), s32[]{:S(2)}) async-start(), calls=%async_computation.13 | async-start | bytes 3481600 | tf_op jit(solution)/shard_map/all_gather | solution.py:28
  12.3 90.6 %all-gather.17.cloned.1.call-start = ((), (), s32[]{:S(2)}) async-start(), calls=%async_computation.14 | async-start | bytes 3481600 | tf_op jit(solution)/shard_map/all_gather | solution.py:28
  15.0 107.9 %all-gather.21.cloned.1.call-start = ((), (), s32[]{:S(2)}) async-start(), calls=%async_computation.16 | async-start | bytes 3481600 | tf_op jit(solution)/shard_map/all_gather | solution.py:28
  15.5 134.8 %all-gather.23.cloned.1.call-start = ((), (), s32[]{:S(2)}) async-start(), calls=%async_computation.17 | async-start | bytes 3481600 | tf_op jit(solution)/shard_map/all_gather | solution.py:28
  16.1 162.4 %all-gather.19.cloned.1.call-start = ((), (), s32[]{:S(2)}) async-start(), calls=%async_computation.15 | async-start | bytes 3481600 | tf_op jit(solution)/shard_map/all_gather | solution.py:28
  16.7 469.3 %reduce-scatter.15.cloned.1.call-start = ((), (), s32[]{:S(2)}) async-start(), calls=%async_computation.10 | async-start | bytes 3481600 | tf_op jit(solution)/shard_map/reduce_scatter | solution.py:31
  28.2 0.6 copy-start
  28.8 38.0 %copy-start.2 = (f32[4096]{0:T(1024)}, f32[4096]{0:T(1024)S(1)}, u32[]{:S(2)}) copy-start(f32[4096]{0:T(1024)S(1)} %fusion.58) | copy-start | bytes 49156
  122.8 21.2 %copy-start.6 = (f32[4096]{0:T(1024)}, f32[4096]{0:T(1024)S(1)}, u32[]{:S(2)}) copy-start(f32[4096]{0:T(1024)S(1)} %get-tuple-element.22) | copy-start | bytes 49156
  122.8 148.5 %copy-start.4 = (f32[4096]{0:T(1024)}, f32[4096]{0:T(1024)S(1)}, u32[]{:S(2)}) copy-start(f32[4096]{0:T(1024)S(1)} %fusion.59) | copy-start | bytes 49156
  226.0 18.5 %copy-start.10 = (bf16[1,640,2176]{2,1,0:T(8,128)(2,1)S(1)}, bf16[1,640,2176]{2,1,0:T(8,128)(2,1)}, u32[]{:S(2)}) copy-start(bf16[1,640,2176]{2,1,0:T(8,128)(2,1)} %all-gather.23.cloned.1.call-done) | copy-start | bytes 8355844
  244.6 26.8 %copy-start.7 = (f32[4096]{0:T(1024)S(1)}, f32[4096]{0:T(1024)}, u32[]{:S(2)}) copy-start(f32[4096]{0:T(1024)} %copy-done.6) | copy-start | bytes 49156
  304.2 29.6 %copy-start.9 = (bf16[1,2176,640]{2,1,0:T(8,128)(2,1)S(1)}, bf16[1,2176,640]{2,1,0:T(8,128)(2,1)}, u32[]{:S(2)}) copy-start(bf16[1,2176,640]{2,1,0:T(8,128)(2,1)} %all-gather.17.cloned.1.call-done) | copy-start | bytes 8355844
  304.2 181.8 %reduce-scatter.17.cloned.1.call-start = ((), (), s32[]{:S(2)}) async-start(), calls=%async_computation.11 | async-start | bytes 3481600 | tf_op jit(solution)/shard_map/reduce_scatter | solution.py:31
  333.8 152.3 %reduce-scatter.11.cloned.1.call-start = ((), (), s32[]{:S(2)}) async-start(), calls=%async_computation.8 | async-start | bytes 3481600 | tf_op jit(solution)/shard_map/reduce_scatter | solution.py:31
  333.8 46.8 %copy-start.3 = (f32[4096]{0:T(1024)S(1)}, f32[4096]{0:T(1024)}, u32[]{:S(2)}) copy-start(f32[4096]{0:T(1024)} %copy-done.2) | copy-start | bytes 49156
  380.6 25.1 %copy-start.5 = (f32[4096]{0:T(1024)S(1)}, f32[4096]{0:T(1024)}, u32[]{:S(2)}) copy-start(f32[4096]{0:T(1024)} %copy-done.4) | copy-start | bytes 49156
  405.7 80.3 %reduce-scatter.13.cloned.1.call-start = ((), (), s32[]{:S(2)}) async-start(), calls=%async_computation.9 | async-start | bytes 3481600 | tf_op jit(solution)/shard_map/reduce_scatter | solution.py:31
  430.9 85.8 %reduce-scatter.9.cloned.1.call-start = ((), (), s32[]{:S(2)}) async-start(), calls=%async_computation.7 | async-start | bytes 3481600 | tf_op jit(solution)/shard_map/reduce_scatter | solution.py:31
  449.0 105.4 %reduce-scatter.7.cloned.1.call-start = ((), (), s32[]{:S(2)}) async-start(), calls=%async_computation.6 | async-start | bytes 3481600 | tf_op jit(solution)/shard_map/reduce_scatter | solution.py:31
  467.1 87.3 %copy-start.8 = (bf16[1,640,2176]{2,1,0:T(8,128)(2,1)S(1)}, bf16[1,640,2176]{2,1,0:T(8,128)(2,1)}, u32[]{:S(2)}) copy-start(bf16[1,640,2176]{2,1,0:T(8,128)(2,1)} %all-gather.15.cloned.1.call-done) | copy-start | bytes 8355844
  467.1 246.6 %all-reduce.3.cloned.1.call-start = ((), (), s32[]{:S(2)}) async-start(), calls=%async_computation.18 | async-start | bytes 8355840 | tf_op jit(solution)/shard_map/psum | solution.py:31
  554.5 27.0 %copy-start.1 = (f32[4096]{0:T(1024)S(1)}, f32[4096]{0:T(1024)}, u32[]{:S(2)}) copy-start(f32[4096]{0:T(1024)} %copy-done) | copy-start | bytes 49156
Sparse Core Ops, SparseCore 0:
  10.1 28.8 all-gather.12
  40.6 26.1 all-gather.14
  68.3 26.1 all-gather.16
  96.0 26.1 all-gather.20
  124.1 26.1 all-gather.22
  152.3 26.1 all-gather.18
  304.4 35.2 reduce-scatter.14
  342.2 35.2 reduce-scatter.16
  405.8 35.2 reduce-scatter.10
  443.5 35.2 reduce-scatter.12
  481.4 35.2 reduce-scatter.8
  519.1 35.2 reduce-scatter.6
  558.8 154.9 all-reduce.2
where the time goes:
time: 735 us; the launch traced here: 727 us
  matrix products  447 us (61%)
  waiting for transfers between devices  199 us (27%)
  other arithmetic  33.7 us (5%)
  local copies, waits for them, and re-layouts  31.9 us (4%)
  between operations  14.6 us (2%)
    dot_general x6, matrix products, layer(): up = jnp.dot(a, w['w_up'], preferred_element_type=jnp.float32)  164 us
    dot_general x6, matrix products, layer(): gate = jnp.dot(a, w['w_gate'], preferred_element_type=jnp.float32)  145 us
    dot_general x5, matrix products, matmul(): jnp.dot(a, w, preferred_element_type=jnp.float32).astype(jnp.bfloat16)  138 us
    psum x1, waiting for transfers between devices, summed(): lax.psum(lax.psum_scatter(term, 's', scatter_dimension=0, tiled=True), 'r')  113 us
    reduce_scatter x6, waiting for transfers between devices, summed(): lax.psum_scatter(term, 's', scatter_dimension=0, tiled=True)  68.4 us
    unnamed x25, local copies, waits for them, and re-layouts  24.4 us
    all_gather x6, waiting for transfers between devices, fetched(): lax.all_gather(w[number], 's', axis=0, tiled=True)  16.8 us
  transfers between devices with their start and end apart: 13, of which 7 were waited for; matrix products, arithmetic and copies ran while one was open for 52% of the time, Pallas kernels for 0%

commit v1 on v0

v1 whole, which is shorter than its diff:
```python
import functools
import jax
import jax.numpy as jnp
from jax import lax
from jax.experimental import pallas as pl
from jax.experimental.pallas import tpu as pltpu
from jax.sharding import PartitionSpec as P

T, D, F, EPS = 4096, 640, 2176, 1e-6
BF, F32 = jnp.bfloat16, jnp.float32
TT = 512
CH = [(i * 256, 256) for i in range(8)] + [(2048, 128)]
ANY = pl.BlockSpec(memory_space=pl.ANY)
NT = (((1,), (1,)), ((), ()))


def dot(a, b):
    return jnp.dot(a, b, preferred_element_type=F32)


def dot_nt(a, b):
    return lax.dot_general(a, b, NT, preferred_element_type=F32)


def params(limit=60):
    return pltpu.CompilerParams(vmem_limit_bytes=limit * 2**20)


def cost(flops, nbytes):
    return pl.CostEstimate(flops=int(flops), bytes_accessed=int(nbytes), transcendentals=0)


def norm_of(h):
    wide = h.astype(F32)
    scale = lax.rsqrt(jnp.mean(wide * wide, -1, keepdims=True) + EPS)
    return wide, scale


def sigmoid(g):
    return 1.0 / (1.0 + jnp.exp(-g))


def grads_of(g, u, dact):
    sig = sigmoid(g)
    silu = g * sig
    act = (silu * u).astype(BF)
    dup = dact * silu
    dgate = dact * u * (sig + silu * (1.0 - sig))
    return act, dgate.astype(BF), dup.astype(BF)


def norm_back(da, wide, scale, dy):
    da = da.astype(BF).astype(F32)
    inner = jnp.mean(da * wide, -1, keepdims=True)
    dwide = scale * da - wide * (scale * scale * scale * inner)
    return (dy.astype(F32) + dwide.astype(BF).astype(F32)).astype(BF)


CORE, X, Z1, Z2, Y = range(5)
MESH = pl.DeviceIdType.MESH


def places():
    rep, r, s = lax.axis_index("rep"), lax.axis_index("r"), lax.axis_index("s")
    y, z, x, core = r // 4, r % 4, s // 2, s % 2
    at = lambda y, z, x, core: (rep, y * 4 + z, x * 2 + core)
    low, high = z % 2, z // 2
    partners = [
        at(y, z, x, 1 - core),
        at(y, z, 1 - x, core),
        at(y, high * 2 + 1 - low, x, core),
        at(y, (1 - high) * 2 + low, x, core),
        at(1 - y, z, x, core),
    ]
    return y, low, x, core, s, partners


def greet(partners):
    barrier = pltpu.get_barrier_semaphore()
    for partner in partners:
        pl.semaphore_signal(barrier, inc=1, device_id=partner, device_id_type=MESH)
    pl.semaphore_wait(barrier, len(partners))


def remote(src, dst, send, recv, partner):
    return pltpu.make_async_remote_copy(src_ref=src, dst_ref=dst, send_sem=send, recv_sem=recv, device_id=partner, device_id_type=MESH)


def k1(x_ref, wg, wu, wd, gate_ref, up_ref, act_ref, actt_ref, at_ref, og, ou, od, wgu, sg, su, sd, send, recv, local):
    i = pl.program_id(0)
    y, low, x, core, s, partners = places()
    tensors = [(w, o, stage, layer, rows) for layer in range(2) for w, o, stage, rows in ((wg, og, sg, 160), (wu, ou, su, 160), (wd, od, sd, 544))]

    def copy(k, kind):
        w, o, _, layer, rows = tensors[k]
        half = rows // 2
        across = jnp.bitwise_xor(s, 2)
        own = lambda n, at: o.at[layer, pl.ds(pl.multiple_of(at, 16), n)]
        if kind == 0:
            src, dst, partner = w.at[layer], own(rows, s * rows), CORE
        elif kind == 1:
            src, dst, partner = w.at[layer, pl.ds(pl.multiple_of(y * half, 16), half)], own(half, s * rows + y * half), X
        elif kind in (2, 3):
            src = own(half, across * rows + y * half)
            dst, partner = src, Y if kind == 2 else CORE
        else:
            src = own(half, across * rows + (1 - y) * half)
            dst, partner = src, CORE
        return remote(src, dst, send.at[k, kind], recv.at[k, kind], partners[partner])

    def stage_in(k):
        w, _, stage, layer, _ = tensors[k]
        return pltpu.make_async_copy(w.at[layer], stage.at[layer], local.at[k, 0])

    def stage_out(k):
        _, o, stage, layer, rows = tensors[k]
        return pltpu.make_async_copy(stage.at[layer], o.at[layer, pl.ds(pl.multiple_of(s * rows, 32), rows)], local.at[k, 1])

    def forward_x(k):
        copy(k, 1).wait_recv()
        copy(k, 2).start()
        copy(k, 3).start()

    def forward_y(k):
        copy(k, 2).wait_recv()
        copy(k, 4).start()

    @pl.when(i == 0)
    def _():
        greet([partners[CORE], partners[X], partners[Y]])
        copy(0, 1).start()
        copy(1, 1).start()
        copy(0, 0).start()
        copy(1, 0).start()
        for k in range(6):
            stage_in(k).start()
        for k in range(6):
            stage_in(k).wait()
            stage_out(k).start()
        forward_x(0)
        copy(2, 1).start()
        forward_x(1)
        for k in range(3, 6):
            copy(k, 1).start()
        forward_y(0)
        forward_y(1)
        for k in range(2):
            stage_out(k).wait()
            for kind in (0, 3, 4):
                copy(k, kind).wait_recv()
        loads = [pltpu.make_async_copy(o.at[0], wgu.at[:, pl.ds(c, F)], local.at[c // F, 0]) for o, c in ((og, 0), (ou, F))]
        for load in loads:
            load.start()
        for k in range(2, 6):
            copy(k, 0).start()
        for load in loads:
            load.wait()

    for when, todo in {1: ((forward_x, 2),), 3: ((forward_x, 3), (forward_y, 2)), 4: ((forward_x, 4), (forward_y, 3)), 6: ((forward_x, 5), (forward_y, 4))}.items():

        @pl.when(i == when)
        def _(todo=todo):
            for f, k in todo:
                f(k)

    wide, scale = norm_of(x_ref[...])
    a = (wide * scale).astype(BF)
    at_ref[...] = a.T
    for c, n in CH:
        g = dot(a, wgu[:, c : c + n])
        u = dot(a, wgu[:, F + c : F + c + n])
        gate_ref[:, c : c + n] = g
        up_ref[:, c : c + n] = u
        act = (g * sigmoid(g) * u).astype(BF)
        act_ref[:, c : c + n] = act
        actt_ref[c : c + n, :] = act.T

    @pl.when(i == pl.num_programs(0) - 1)
    def _():
        forward_y(5)
        for k in range(6):
            if k >= 2:
                stage_out(k).wait()
                for kind in (0, 3, 4):
                    copy(k, kind).wait_recv()
            for kind in range(5):
                copy(k, kind).wait_send()


def tile_of(tt):
    return lambda w: pl.BlockSpec((tt, w), lambda i: (i, 0))


def turned_of(tt):
    return lambda w: pl.BlockSpec((w, tt), lambda i: (0, i))


def shape(*dims, dtype=BF):
    return jax.ShapeDtypeStruct(dims, dtype)


def forward0(x, w_gate, w_up, w_down):
    tile, turned = tile_of(TT), turned_of(TT)
    return pl.pallas_call(
        k1,
        grid=(T // TT,),
        in_specs=[tile(D)] + [ANY] * 3,
        out_specs=[tile(F), tile(F), tile(F), turned(F), turned(D)] + [ANY] * 3,
        out_shape=[shape(T, F, dtype=F32)] * 2 + [shape(T, F), shape(F, T), shape(D, T), shape(2, D, F), shape(2, D, F), shape(2, F, D)],
        scratch_shapes=[
            pltpu.VMEM((D, 2 * F), BF),
            pltpu.VMEM((2, D // 4, F), BF),
            pltpu.VMEM((2, D // 4, F), BF),
            pltpu.VMEM((2, F // 4, D), BF),
            pltpu.SemaphoreType.DMA((6, 5)),
            pltpu.SemaphoreType.DMA((6, 5)),
            pltpu.SemaphoreType.DMA((6, 2)),
        ],
        compiler_params=pltpu.CompilerParams(vmem_limit_bytes=60 * 2**20, collective_id=0, has_side_effects=True),
        cost_estimate=cost(4 * T * D * F, 110e6),
        name="forward0",
    )(x, w_gate, w_up, w_down)


def k2(x_ref, act0_ref, dy_ref, wg, wu, wdn, dh_ref, at_ref, actt_ref, dgu_ref, wgu, wd, wd0, sem):
    @pl.when(pl.program_id(0) == 0)
    def _():
        copies = [
            pltpu.make_async_copy(wdn.at[0], wd0, sem.at[0]),
            pltpu.make_async_copy(wg.at[1], wgu.at[:, pl.ds(0, F)], sem.at[1]),
            pltpu.make_async_copy(wu.at[1], wgu.at[:, pl.ds(F, F)], sem.at[2]),
            pltpu.make_async_copy(wdn.at[1], wd, sem.at[3]),
        ]
        for c in copies:
            c.start()
        for c in copies:
            c.wait()

    h = (x_ref[...].astype(F32) + dot(act0_ref[...], wd0[...]).astype(BF).astype(F32)).astype(BF)
    wide, scale = norm_of(h)
    a = (wide * scale).astype(BF)
    dy = dy_ref[...]
    at_ref[...] = a.T
    for c, n in CH:
        g = dot(a, wgu[:, c : c + n])
        u = dot(a, wgu[:, F + c : F + c + n])
        dact = dot_nt(dy, wd[c : c + n, :]).astype(BF).astype(F32)
        act, dgate, dup = grads_of(g, u, dact)
        actt_ref[c : c + n, :] = act.T
        dgu_ref[:, c : c + n] = dgate
        dgu_ref[:, F + c : F + c + n] = dup
    dh_ref[...] = norm_back(dot_nt(dgu_ref[...], wgu[...]), wide, scale, dy)


def layer1(x, act0, dy, wg, wu, wd):
    tile, turned = tile_of(TT), turned_of(TT)
    return pl.pallas_call(
        k2,
        grid=(T // TT,),
        in_specs=[tile(D), tile(F), tile(D)] + [ANY] * 3,
        out_specs=[tile(D), turned(D), turned(F), tile(2 * F)],
        out_shape=[shape(T, D), shape(D, T), shape(F, T), shape(T, 2 * F)],
        scratch_shapes=[pltpu.VMEM((D, 2 * F), BF), pltpu.VMEM((F, D), BF), pltpu.VMEM((F, D), BF), pltpu.SemaphoreType.DMA((4,))],
        compiler_params=params(),
        cost_estimate=cost(12 * T * D * F, 100e6),
        name="layer1",
    )(x, act0, dy, wg, wu, wd)


def k4(dh_ref, gate_ref, up_ref, wdn, dgu_ref, wd, sem):
    @pl.when(pl.program_id(0) == 0)
    def _():
        c = pltpu.make_async_copy(wdn.at[0], wd, sem)
        c.start()
        c.wait()

    dy = dh_ref[...]
    for c, n in CH:
        dact = dot_nt(dy, wd[c : c + n, :]).astype(BF).astype(F32)
        _, dgate, dup = grads_of(gate_ref[:, c : c + n], up_ref[:, c : c + n], dact)
        dgu_ref[:, c : c + n] = dgate
        dgu_ref[:, F + c : F + c + n] = dup


def backward0(dh, gate, up, wd):
    tile = tile_of(256)
    return pl.pallas_call(
        k4,
        grid=(T // 256,),
        in_specs=[tile(D), tile(F), tile(F), ANY],
        out_specs=tile(2 * F),
        out_shape=shape(T, 2 * F),
        scratch_shapes=[pltpu.VMEM((F, D), BF), pltpu.SemaphoreType.DMA],
        compiler_params=params(),
        cost_estimate=cost(2 * T * D * F, 112e6),
        name="backward0",
    )(dh, gate, up, wd)


NA, NB, AB = 34, 12, 46
STEPS, TC = 62, 256


class Stream:
    def __init__(self, bufs, sems, slots, lags, piece_at, put):
        self.own, self.rd, self.s1, self.rx, self.s2, self.ry, self.s3, self.rz, self.s4, self.rq, self.fin = bufs
        self.send, self.recv = sems
        self.slots, self.lags, self.piece_at, self.put = slots, lags, piece_at, put

    def copies(self, c, at):
        y, low, x, core, _, partners = at
        e, n = c % 4, c % self.slots
        def make(p, src, dst, partner, slot):
            return remote(src, dst, self.send.at[p, slot], self.recv.at[p, slot], partners[partner])
        return [
            lambda: make(0, self.own.at[e, 1 - core], self.rd.at[e], CORE, e),
            lambda: make(1, self.s1.at[n, 1 - x], self.rx.at[n], X, n),
            lambda: make(2, self.s2.at[n, 1 - y], self.ry.at[n], Y, n),
            lambda: make(3, self.s3.at[n, 1 - low], self.rz.at[n], Z1, n),
            lambda: make(4, self.s4.at[n], self.rq.at[n], Z2, n),
            lambda: make(5, self.fin.at[n, y, low], self.fin.at[n, y, low], Z1, n),
            lambda: make(6, self.fin.at[n, y], self.fin.at[n, y], Y, n),
        ]

    def add(self, stage, c, at):
        y, low, x, core, _, _ = at
        e, n = c % 4, c % self.slots
        wide = lambda v: v.astype(F32)
        if stage == 1:
            self.s1[n] = (wide(self.own[e, core]) + wide(self.rd[e])).astype(BF)
        if stage == 2:
            self.s2[n] = (wide(self.s1[n, x]) + wide(self.rx[n])).astype(BF)
        if stage == 3:
            self.s3[n] = (wide(self.s2[n, y]) + wide(self.ry[n])).astype(BF)
        if stage == 4:
            self.s4[n] = (wide(self.s3[n, low]) + wide(self.rz[n])).astype(BF)
        if stage == 5:
            self.fin[n, y, low] = (wide(self.s4[n]) + wide(self.rq[n])).astype(BF)

    def advance(self, i, at):
        for stage in range(8, 0, -1):
            valid, c = self.piece_at(i - self.lags[stage])

            @pl.when(valid)
            def _(stage=stage, c=c):
                copies = self.copies(c, at)
                if stage == 8:
                    for copy in self.put(c, self.fin, c % self.slots):
                        copy.wait()
                    return
                copies[stage - 1]().wait()
                self.add(stage, c, at)
                if stage == 7:
                    for copy in self.put(c, self.fin, c % self.slots):
                        copy.start()
                else:
                    copies[stage]().start()


def piece_a(j):
    return (j >= 0) & (j < AB) & (j % 4 != 0), 3 * (j // 4) + j % 4 - 1


def piece_b(j):
    return (j >= 0) & (j < AB) & (j % 4 == 0), j // 4


LAGS_A = (0, 1, 4, 6, 8, 10, 12, 14, 15)
LAGS_B = (0, 1, 5, 8, 10, 12, 14, 16, 17)


def row_of(c):
    return pl.multiple_of(jnp.minimum(c % 6 * 96, 448), 32)


def k5(dgu1_ref, dgu0_ref, x_ref, dht_ref, tile_ref, dy, dh, at1, at0, actt1, actt0, wg, wu, dx_ref, out_gu, out_d, *rest):
    abufs, bbufs, rest = rest[:11], rest[11:22], rest[22:]
    (asend, arecv, bsend, brecv, aput, bput, big0, big1, lt1, lt0, lhs, wgu, sem, lsem) = rest
    i = pl.program_id(0)
    at = places()

    def put_a(c, fin, n):
        where = out_gu.at[1 - c // 17, :, :, :, pl.ds(pl.multiple_of(c % 17 * 256, 256), 256)]
        return [pltpu.make_async_copy(fin.at[n], where, aput.at[n])]

    def put_b(c, fin, n):
        row = row_of(c)
        return [pltpu.make_async_copy(fin.at[n, q // 2, q % 2], out_d.at[1 - c // 6, pl.ds(pl.multiple_of(row + 24 * q, 8), 24)], bput.at[n, q]) for q in range(4)]

    a = Stream(abufs, (asend, arecv), 6, LAGS_A, piece_a, put_a)
    b = Stream(bbufs, (bsend, brecv), 4, LAGS_B, piece_b, put_b)

    load = [
        pltpu.make_async_copy(dy, big1, sem.at[0]),
        pltpu.make_async_copy(at1, lt1, sem.at[1]),
        pltpu.make_async_copy(at0, lt0, sem.at[2]),
        pltpu.make_async_copy(dh, big0, sem.at[3]),
        pltpu.make_async_copy(wg.at[0], wgu.at[:, pl.ds(0, F)], sem.at[4]),
        pltpu.make_async_copy(wu.at[0], wgu.at[:, pl.ds(F, F)], sem.at[5]),
    ]

    def lhs_copies(c, source):
        row = row_of(c)
        return [pltpu.make_async_copy(source.at[pl.ds(pl.multiple_of(544 * q + row, 32), 96)], lhs.at[c % 2, pl.ds(96 * q, 96)], lsem.at[c % 2, q]) for q in range(4)]

    def fetch_lhs(c):
        @pl.when(c < 6)
        def _():
            for copy in lhs_copies(c, actt1):
                copy.start()

        @pl.when((c >= 6) & (c < NB))
        def _():
            for copy in lhs_copies(c, actt0):
                copy.start()

    @pl.when(i == 0)
    def _():
        fetch_lhs(0 * i)
        for copy in load:
            copy.start()
        greet(at[5])
        load[0].wait()

    for when, which in {1: (1,), 23: (2,), 24: (3,), AB: (4, 5)}.items():

        @pl.when(i == when)
        def _(which=which):
            for w in which:
                load[w].wait()

    a.advance(i, at)
    b.advance(i, at)

    is_a, ca = piece_a(i)
    is_b, cb = piece_b(i)

    def weight_a(lt, r):
        out = dot(lt[...], r[...])
        for q in range(4):
            a.own[ca % 4, q % 2, q // 2] = out[160 * q : 160 * q + 160].reshape(2, 2, 40, 256).astype(BF)
        a.copies(ca, at)[0]().start()

    def weight_b(big):
        for copy in lhs_copies(cb, actt1):
            copy.wait()
        fetch_lhs(cb + 1)
        out = dot(lhs[cb % 2], big[...])
        for q in range(4):
            b.own[cb % 4, q % 2, q // 2] = out[96 * q : 96 * q + 96].reshape(2, 2, 24, D).astype(BF)
        b.copies(cb, at)[0]().start()

    pl.when(is_a & (ca < 17))(lambda: weight_a(lt1, dgu1_ref))
    pl.when(is_a & (ca >= 17))(lambda: weight_a(lt0, dgu0_ref))
    pl.when(is_b & (cb < 6))(lambda: weight_b(big1))
    pl.when(is_b & (cb >= 6))(lambda: weight_b(big0))

    @pl.when(i >= AB)
    def _():
        wide, scale = norm_of(x_ref[...])
        dx_ref[...] = norm_back(dot_nt(tile_ref[...], wgu[...]), wide, scale, dht_ref[...])


def weights_and_input(x, dy, dh, at1, at0, actt1, actt0, dgu1, dgu0, wg, wu):
    def piece(first):
        def index(i):
            j = jnp.minimum(i, AB - 1)
            return (0, jnp.clip(3 * (j // 4) + jnp.maximum(j % 4 - 1, 0) - first, 0, 16))
        return index
    tile = lambda w: pl.BlockSpec((TC, w), lambda i: (jnp.maximum(i - AB, 0), 0))

    def bufs(own_slots, n, r, c):
        v = lambda *dims: pltpu.VMEM(dims + (r, c), BF)
        return [v(4, 2, 2, 2, 2), v(4, 2, 2, 2), v(n, 2, 2, 2), v(n, 2, 2), v(n, 2, 2), v(n, 2), v(n, 2), v(n), v(n), v(n), v(n, 2, 2)]

    dma = pltpu.SemaphoreType.DMA
    return pl.pallas_call(
        k5,
        grid=(STEPS,),
        in_specs=[pl.BlockSpec((T, 256), piece(0)), pl.BlockSpec((T, 256), piece(17)), tile(D), tile(D), tile(2 * F)] + [ANY] * 8,
        out_specs=[tile(D), ANY, ANY],
        out_shape=[shape(T, D), shape(2, 2, 2, 40, 2 * F), shape(2, F // 4, D)],
        scratch_shapes=bufs(4, 6, 40, 256)
        + bufs(4, 4, 24, D)
        + [dma((7, 6)), dma((7, 6)), dma((7, 4)), dma((7, 4)), dma((6,)), dma((4, 4))]
        + [pltpu.VMEM((T, D), BF), pltpu.VMEM((T, D), BF), pltpu.VMEM((D, T), BF), pltpu.VMEM((D, T), BF)]
        + [pltpu.VMEM((2, 384, T), BF), pltpu.VMEM((D, 2 * F), BF), dma((6,)), dma((2, 4))],
        compiler_params=pltpu.CompilerParams(vmem_limit_bytes=67043328, collective_id=1, has_side_effects=True),
        cost_estimate=cost(16 * T * D * F, 150e6),
        name="weights_and_input",
    )(dgu1, dgu0, x, dh, dgu0, dy, dh, at1, at0, actt1, actt0, wg, wu)


def solution(mesh):
    def step(x, dy, w_gate, w_up, w_down):
        x, dy = x[0], dy[0]
        gate, up, act0, actt0, at0, wg, wu, wd = forward0(x, w_gate, w_up, w_down)
        dh, at1, actt1, dgu1 = layer1(x, act0, dy, wg, wu, wd)
        dgu0 = backward0(dh, gate, up, wd)
        dx, gu, down = weights_and_input(x, dy, dh, at1, at0, actt1, actt0, dgu1, dgu0, wg, wu)
        gu = gu.reshape(2, D // 4, 2 * F)
        return dx[None], gu[:, :, :F], gu[:, :, F:], down

    states, cut = P(("rep", "r", "s"), None, None), P(None, "s", None)
    return jax.shard_map(
        step,
        mesh=mesh,
        in_specs=(states, states) + (cut,) * 3,
        out_specs=(states,) + (P("rep", "s", None),) * 3,
        check_vma=False,
    )
```

time: 735 us -> 448 us (0.61); the launches traced: 727 us -> 448 us
  matrix products: 447 us -> 0 us
  Pallas kernels: 0 us -> 440 us
  waiting for transfers between devices: 199 us -> 0 us
  other arithmetic: 33.7 us -> 0 us
  local copies, waits for them, and re-layouts: 31.9 us -> 7.4 us
  between operations: 14.6 us -> 0.67 us
    dot_general x17 -> x0, matrix products: 447 us -> none  [the longest x6 164 us: layer(): up = jnp.dot(a, w['w_up'], preferred_element_type=jnp.float32)]
    pallas_call x0 -> x4, Pallas kernels: none -> 440 us  [the longest x1 198 us: weights_and_input(): pl.pallas_call(k5, grid=(STEPS,), in_specs=[pl.BlockSpec((T, 256), piece(...]
    psum x1 -> x0, waiting for transfers between devices: 113 us -> none  [summed(): lax.psum(lax.psum_scatter(term, 's', scatter_dimension=0, tiled=True), 'r')]
    reduce_scatter x6 -> x0, waiting for transfers between devices: 68.4 us -> none  [summed(): lax.psum_scatter(term, 's', scatter_dimension=0, tiled=True)]
    unnamed x25 -> x6, local copies, waits for them, and re-layouts: 24.4 us -> 3.75 us
    all_gather x6 -> x0, waiting for transfers between devices: 16.8 us -> none  [fetched(): lax.all_gather(w[number], 's', axis=0, tiled=True)]
    broadcast_in_dim x1 -> x0, other arithmetic: 11.9 us -> none  [step(): by_h[None]]
    add_any x1 -> x0, other arithmetic: 11.9 us -> none  [normed(): wide = h.astype(jnp.float32)]
  transfers between devices with their start and end apart: 13 -> 0, of which waited for: 7 -> 0; matrix products, arithmetic and copies ran while one was open for 52% -> 0% of each run, Pallas kernels for 0% -> 0%
where the time goes in v1:
time: 448 us
  Pallas kernels  440 us (98%)
  local copies, waits for them, and re-layouts  7.4 us (2%)
    pallas_call x1, Pallas kernels, weights_and_input(): pl.pallas_call(k5, grid=(STEPS,), in_specs=[pl.BlockSpec((T, 256), piece(...  198 us
    pallas_call x1, Pallas kernels, layer1(): pl.pallas_call(k2, grid=(T // TT,), in_specs=[tile(D), tile(F), tile(D)]...  114 us
    pallas_call x1, Pallas kernels, forward0(): pl.pallas_call(k1, grid=(T // TT,), in_specs=[tile(D)] + [ANY] * 3, out_s...  80.9 us
    pallas_call x1, Pallas kernels, backward0(): pl.pallas_call(k4, grid=(T // 256,), in_specs=[tile(D), tile(F), tile(F),...  46.6 us

profile of v1, /device:TPU:0, one launch (start us, length us, event | category | flops | bytes accessed | tf_op | source)
XLA Modules:
  0.0 447.7 jit_solution(17117512069843394162)
XLA Ops:
  0.6 80.9 %forward0.1 = (f32[4096,2176]{1,0:T(8,128)}, f32[4096,2176]{1,0:T(8,128)}, bf16[4096,2176]{1,0:T(8,128)(2,1)}, bf16[2176,4096]{1,0:T(8,128)(2,1)}, bf16[640,4096...) custom-call(bf16[4096,640]{1,0:T(8,128)(2,1)} %bitcast.6, ...), custom_call_target="tpu_custom_call" | custom-call | flops 22817013760 | bytes 110000000 | tf_op jit(solution)/shard_map/forward0/pallas_call | solution.py:204
  81.5 113.6 %layer1.1 = (bf16[4096,640]{1,0:T(8,128)(2,1)}, bf16[640,4096]{1,0:T(8,128)(2,1)}, bf16[2176,4096]{1,0:T(8,128)(2,1)}, bf16[4096,4352]{1,0:T(8,128)(2,1)}) custom-call(bf16[4096,640]{1,0:T(8,128)(2,1)} %bitcast.7, bf16[4096,2176]{1,0:T(8,128)(2,1)} %get-tuple-element.19.act0_ref, bf16[4096,640]{1,0:T(8,128)(2,1)} %bitcast.9, ...), custom_call_target="tpu_custom_call" | custom-call | flops 68451041280 | bytes 100000000 | tf_op jit(solution)/shard_map/layer1/pallas_call | solution.py:257
  195.1 46.6 %backward0.1.dgu0_ref.tile_ref = bf16[4096,4352]{1,0:T(8,128)(2,1)} custom-call(bf16[4096,640]{1,0:T(8,128)(2,1)} %get-tuple-element.24.dh_ref.dht_ref.dh, f32[4096,2176]{1,0:T(8,128)} %get-tuple-element.25.gate_ref, f32[4096,2176]{1,0:T(8,128)} %get-tuple-element.26.up_ref, bf16[2,2176,640]{2,1,0:T(8,128)(2,1)} %get-tuple-element.22.wdn), custom_call_target="tpu_custom_call" | custom-call | flops 11408506880 | bytes 112000000 | tf_op jit(solution)/shard_map/backward0/pallas_call | solution.py:287
  241.8 198.5 %weights_and_input.1 = (bf16[4096,640]{1,0:T(8,128)(2,1)}, bf16[2,2,2,40,4352]{4,3,2,1,0:T(8,128)(2,1)}, bf16[2,544,640]{2,1,0:T(8,128)(2,1)}) custom-call(bf16[4096,4352]{1,0:T(8,128)(2,1)} %get-tuple-element.23.dgu1_ref, bf16[4096,4352]{1,0:T(8,128)(2,1)} %backward0.1.dgu0_ref.tile_ref, bf16[4096,640]{1,0:T(8,128)(2,1)} %bitcast.8, ...), custom_call_target="tpu_custom_call" | custom-call | flops 91268055040 | bytes 150000000 | tf_op jit(solution)/shard_map/weights_and_input/pallas_call | solution.py:477
  440.3 0.0 copy-start
  440.3 3.7 fusion
  443.9 0.3 copy-done
  444.2 0.0 copy-start.1
  444.2 2.4 copy.11
  446.6 0.0 copy-done.1
  446.6 1.1 copy.12
Async XLA Ops:
  440.3 4.0 copy-start
  444.2 2.4 copy-start.1

commit v2 on v1

--- a/solution.py
+++ b/solution.py
@@ -236,8 +236,11 @@
         for c in copies:
             c.wait()
 
-    h = (x_ref[...].astype(F32) + dot(act0_ref[...], wd0[...]).astype(BF).astype(F32)).astype(BF)
-    wide, scale = norm_of(h)
+    parts = []
+    for r in range(0, TT, 256):
+        h = (x_ref[r : r + 256, :].astype(F32) + dot(act0_ref[r : r + 256, :], wd0[...]).astype(BF).astype(F32)).astype(BF)
+        parts.append((*norm_of(h),))
+    wide, scale = (jnp.concatenate(p, 0) for p in zip(*parts))
     a = (wide * scale).astype(BF)
     dy = dy_ref[...]
     at_ref[...] = a.T
@@ -249,7 +252,9 @@
         actt_ref[c : c + n, :] = act.T
         dgu_ref[:, c : c + n] = dgate
         dgu_ref[:, F + c : F + c + n] = dup
-    dh_ref[...] = norm_back(dot_nt(dgu_ref[...], wgu[...]), wide, scale, dy)
+    for r in range(0, TT, 256):
+        q = slice(r, r + 256)
+        dh_ref[q, :] = norm_back(dot_nt(wgu[...], dgu_ref[q, :]).T, wide[q], scale[q], dy[q])
 
 
 def layer1(x, act0, dy, wg, wu, wd):
@@ -283,10 +288,10 @@
 
 
 def backward0(dh, gate, up, wd):
-    tile = tile_of(256)
+    tile = tile_of(512)
     return pl.pallas_call(
         k4,
-        grid=(T // 256,),
+        grid=(T // 512,),
         in_specs=[tile(D), tile(F), tile(F), ANY],
         out_specs=tile(2 * F),
         out_shape=shape(T, 2 * F),
@@ -297,21 +302,25 @@
     )(dh, gate, up, wd)
 
 
-NA, NB, AB = 34, 12, 46
+PAIRS, NB, CYCLES = 17, 12, 17
 STEPS, TC = 62, 256
+MIX = 3 * CYCLES
+EARLY = CYCLES - NB
 
 
 class Stream:
-    def __init__(self, bufs, sems, slots, lags, piece_at, put):
+    def __init__(self, bufs, sems, count, first, put):
         self.own, self.rd, self.s1, self.rx, self.s2, self.ry, self.s3, self.rz, self.s4, self.rq, self.fin = bufs
         self.send, self.recv = sems
-        self.slots, self.lags, self.piece_at, self.put = slots, lags, piece_at, put
+        self.count, self.first, self.put = count, first, put
 
     def copies(self, c, at):
         y, low, x, core, _, partners = at
-        e, n = c % 4, c % self.slots
+        e, n = c & 1, c & 3
+
         def make(p, src, dst, partner, slot):
             return remote(src, dst, self.send.at[p, slot], self.recv.at[p, slot], partners[partner])
+
         return [
             lambda: make(0, self.own.at[e, 1 - core], self.rd.at[e], CORE, e),
             lambda: make(1, self.s1.at[n, 1 - x], self.rx.at[n], X, n),
@@ -324,7 +333,7 @@
 
     def add(self, stage, c, at):
         y, low, x, core, _, _ = at
-        e, n = c % 4, c % self.slots
+        e, n = c & 1, c & 3
         wide = lambda v: v.astype(F32)
         if stage == 1:
             self.s1[n] = (wide(self.own[e, core]) + wide(self.rd[e])).astype(BF)
@@ -337,40 +346,28 @@
         if stage == 5:
             self.fin[n, y, low] = (wide(self.s4[n]) + wide(self.rq[n])).astype(BF)
 
-    def advance(self, i, at):
+    def advance(self, cycle, at):
         for stage in range(8, 0, -1):
-            valid, c = self.piece_at(i - self.lags[stage])
-
-            @pl.when(valid)
+            c = cycle - stage + self.first
+
+            @pl.when((c >= 0) & (c < self.count))
             def _(stage=stage, c=c):
                 copies = self.copies(c, at)
                 if stage == 8:
-                    for copy in self.put(c, self.fin, c % self.slots):
+                    for copy in self.put(c, self.fin, c & 3):
                         copy.wait()
                     return
                 copies[stage - 1]().wait()
                 self.add(stage, c, at)
                 if stage == 7:
-                    for copy in self.put(c, self.fin, c % self.slots):
+                    for copy in self.put(c, self.fin, c & 3):
                         copy.start()
                 else:
                     copies[stage]().start()
 
 
-def piece_a(j):
-    return (j >= 0) & (j < AB) & (j % 4 != 0), 3 * (j // 4) + j % 4 - 1
-
-
-def piece_b(j):
-    return (j >= 0) & (j < AB) & (j % 4 == 0), j // 4
-
-
-LAGS_A = (0, 1, 4, 6, 8, 10, 12, 14, 15)
-LAGS_B = (0, 1, 5, 8, 10, 12, 14, 16, 17)
-
-
 def row_of(c):
-    return pl.multiple_of(jnp.minimum(c % 6 * 96, 448), 32)
+    return pl.multiple_of(jnp.minimum((c - jnp.where(c >= 6, 6, 0)) * 96, 448), 32)
 
 
 def k5(dgu1_ref, dgu0_ref, x_ref, dht_ref, tile_ref, dy, dh, at1, at0, actt1, actt0, wg, wu, dx_ref, out_gu, out_d, *rest):
@@ -380,15 +377,20 @@
     at = places()
 
     def put_a(c, fin, n):
-        where = out_gu.at[1 - c // 17, :, :, :, pl.ds(pl.multiple_of(c % 17 * 256, 256), 256)]
-        return [pltpu.make_async_copy(fin.at[n], where, aput.at[n])]
+        copies = []
+        for half in range(2):
+            part = 2 * c + half
+            late = jnp.where(part >= 17, 1, 0)
+            where = out_gu.at[1 - late, :, :, :, pl.ds(pl.multiple_of((part - 17 * late) * 256, 256), 256)]
+            copies.append(pltpu.make_async_copy(fin.at[n, :, :, :, pl.ds(256 * half, 256)], where, aput.at[n, half]))
+        return copies
 
     def put_b(c, fin, n):
         row = row_of(c)
-        return [pltpu.make_async_copy(fin.at[n, q // 2, q % 2], out_d.at[1 - c // 6, pl.ds(pl.multiple_of(row + 24 * q, 8), 24)], bput.at[n, q]) for q in range(4)]
-
-    a = Stream(abufs, (asend, arecv), 6, LAGS_A, piece_a, put_a)
-    b = Stream(bbufs, (bsend, brecv), 4, LAGS_B, piece_b, put_b)
+        return [pltpu.make_async_copy(fin.at[n, q // 2, q % 2], out_d.at[jnp.where(c >= 6, 0, 1), pl.ds(pl.multiple_of(row + 24 * q, 8), 24)], bput.at[n, q]) for q in range(4)]
+
+    a = Stream(abufs, (asend, arecv), PAIRS, 0, put_a)
+    b = Stream(bbufs, (bsend, brecv), NB, 1, put_b)
 
     load = [
         pltpu.make_async_copy(dy, big1, sem.at[0]),
@@ -401,7 +403,7 @@
 
     def lhs_copies(c, source):
         row = row_of(c)
-        return [pltpu.make_async_copy(source.at[pl.ds(pl.multiple_of(544 * q + row, 32), 96)], lhs.at[c % 2, pl.ds(96 * q, 96)], lsem.at[c % 2, q]) for q in range(4)]
+        return [pltpu.make_async_copy(source.at[pl.ds(pl.multiple_of(544 * q + row, 32), 96)], lhs.at[c & 1, pl.ds(96 * q, 96)], lsem.at[c & 1, q]) for q in range(4)]
 
     def fetch_lhs(c):
         @pl.when(c < 6)
@@ -422,32 +424,41 @@
         greet(at[5])
         load[0].wait()
 
-    for when, which in {1: (1,), 23: (2,), 24: (3,), AB: (4, 5)}.items():
+    for when, which in {1: (1,), 18: (3,), 26: (2,), 3 * NB: (4, 5)}.items():
 
         @pl.when(i == when)
         def _(which=which):
             for w in which:
                 load[w].wait()
 
-    a.advance(i, at)
-    b.advance(i, at)
-
-    is_a, ca = piece_a(i)
-    is_b, cb = piece_b(i)
+    cycle = lax.div(i, 3)
+    place = i - 3 * cycle
+    mixed = i < MIX
+    tick = jnp.where(mixed, cycle, i - MIX + CYCLES)
+    pl.when(~mixed | (place == 1))(lambda: a.advance(tick, at))
+    pl.when(~mixed | (place == 2))(lambda: b.advance(tick, at))
+
+    is_a, ca = mixed & (place > 0), 2 * cycle + place - 1
+    is_b, cb = mixed & (place == 0) & (cycle < NB), cycle
 
     def weight_a(lt, r):
         out = dot(lt[...], r[...])
+        pair, half = cycle, place - 1
         for q in range(4):
-            a.own[ca % 4, q % 2, q // 2] = out[160 * q : 160 * q + 160].reshape(2, 2, 40, 256).astype(BF)
-        a.copies(ca, at)[0]().start()
+            part = out[160 * q : 160 * q + 160].reshape(2, 2, 40, 256).astype(BF)
+            a.own[pair & 1, q % 2, q // 2, :, :, :, pl.ds(pl.multiple_of(half * 256, 256), 256)] = part
+
+        @pl.when(half == 1)
+        def _():
+            a.copies(pair, at)[0]().start()
 
     def weight_b(big):
         for copy in lhs_copies(cb, actt1):
             copy.wait()
         fetch_lhs(cb + 1)
-        out = dot(lhs[cb % 2], big[...])
+        out = dot(lhs[cb & 1], big[...])
         for q in range(4):
-            b.own[cb % 4, q % 2, q // 2] = out[96 * q : 96 * q + 96].reshape(2, 2, 24, D).astype(BF)
+            b.own[cb & 1, q % 2, q // 2] = out[96 * q : 96 * q + 96].reshape(2, 2, 24, D).astype(BF)
         b.copies(cb, at)[0]().start()
 
     pl.when(is_a & (ca < 17))(lambda: weight_a(lt1, dgu1_ref))
@@ -455,23 +466,29 @@
     pl.when(is_b & (cb < 6))(lambda: weight_b(big1))
     pl.when(is_b & (cb >= 6))(lambda: weight_b(big0))
 
-    @pl.when(i >= AB)
+    @pl.when(~mixed | ((place == 0) & (cycle >= NB)))
     def _():
         wide, scale = norm_of(x_ref[...])
-        dx_ref[...] = norm_back(dot_nt(tile_ref[...], wgu[...]), wide, scale, dht_ref[...])
+        dx_ref[...] = norm_back(dot_nt(wgu[...], tile_ref[...]).T, wide, scale, dht_ref[...])
 
 
 def weights_and_input(x, dy, dh, at1, at0, actt1, actt0, dgu1, dgu0, wg, wu):
     def piece(first):
         def index(i):
-            j = jnp.minimum(i, AB - 1)
-            return (0, jnp.clip(3 * (j // 4) + jnp.maximum(j % 4 - 1, 0) - first, 0, 16))
+            j = jnp.minimum(i, MIX - 1)
+            part = 2 * (j // 3) + jnp.maximum(j % 3 - 1, 0)
+            return (0, jnp.clip(part - first, 0, 16))
+
         return index
-    tile = lambda w: pl.BlockSpec((TC, w), lambda i: (jnp.maximum(i - AB, 0), 0))
-
-    def bufs(own_slots, n, r, c):
+
+    def index(i):
+        return (jnp.where(i < MIX, jnp.clip(i // 3 - NB, 0, EARLY - 1), i - MIX + EARLY), 0)
+
+    tile = lambda w: pl.BlockSpec((TC, w), index)
+
+    def bufs(n, r, c):
         v = lambda *dims: pltpu.VMEM(dims + (r, c), BF)
-        return [v(4, 2, 2, 2, 2), v(4, 2, 2, 2), v(n, 2, 2, 2), v(n, 2, 2), v(n, 2, 2), v(n, 2), v(n, 2), v(n), v(n), v(n), v(n, 2, 2)]
+        return [v(2, 2, 2, 2, 2), v(2, 2, 2, 2), v(n, 2, 2, 2), v(n, 2, 2), v(n, 2, 2), v(n, 2), v(n, 2), v(n), v(n), v(n), v(n, 2, 2)]
 
     dma = pltpu.SemaphoreType.DMA
     return pl.pallas_call(
@@ -480,9 +497,9 @@
         in_specs=[pl.BlockSpec((T, 256), piece(0)), pl.BlockSpec((T, 256), piece(17)), tile(D), tile(D), tile(2 * F)] + [ANY] * 8,
         out_specs=[tile(D), ANY, ANY],
         out_shape=[shape(T, D), shape(2, 2, 2, 40, 2 * F), shape(2, F // 4, D)],
-        scratch_shapes=bufs(4, 6, 40, 256)
-        + bufs(4, 4, 24, D)
-        + [dma((7, 6)), dma((7, 6)), dma((7, 4)), dma((7, 4)), dma((6,)), dma((4, 4))]
+        scratch_shapes=bufs(4, 40, 512)
+        + bufs(4, 24, D)
+        + [dma((7, 4)), dma((7, 4)), dma((7, 4)), dma((7, 4)), dma((4, 2)), dma((4, 4))]
         + [pltpu.VMEM((T, D), BF), pltpu.VMEM((T, D), BF), pltpu.VMEM((D, T), BF), pltpu.VMEM((D, T), BF)]
         + [pltpu.VMEM((2, 384, T), BF), pltpu.VMEM((D, 2 * F), BF), dma((6,)), dma((2, 4))],
         compiler_params=pltpu.CompilerParams(vmem_limit_bytes=67043328, collective_id=1, has_side_effects=True),

time: 448 us -> 396 us (0.88)
  Pallas kernels: 440 us -> 388 us
    pallas_call x1, Pallas kernels: 198 us -> 163 us  [weights_and_input(): pl.pallas_call(k5, grid=(STEPS,), in_specs=[pl.BlockSpec((T, 256), piece(...]
    pallas_call x1, Pallas kernels: 114 us -> 100 us  [layer1(): pl.pallas_call(k2, grid=(T // TT,), in_specs=[tile(D), tile(F), tile(D)]...]
where the time goes in v2:
time: 396 us
  Pallas kernels  388 us (98%)
  local copies, waits for them, and re-layouts  7.4 us (2%)
    pallas_call x1, Pallas kernels, weights_and_input(): pl.pallas_call(k5, grid=(STEPS,), in_specs=[pl.BlockSpec((T, 256), piece(...  163 us
    pallas_call x1, Pallas kernels, layer1(): pl.pallas_call(k2, grid=(T // TT,), in_specs=[tile(D), tile(F), tile(D)]...  100 us
    pallas_call x1, Pallas kernels, forward0(): pl.pallas_call(k1, grid=(T // TT,), in_specs=[tile(D)] + [ANY] * 3, out_s...  80.9 us
    pallas_call x1, Pallas kernels, backward0(): pl.pallas_call(k4, grid=(T // 512,), in_specs=[tile(D), tile(F), tile(F),...  43.9 us

profile of v2, /device:TPU:0, one launch (start us, length us, event | category | flops | bytes accessed | tf_op | source)
XLA Modules:
  0.0 396.2 jit_solution(6244324865106615976)
XLA Ops:
  0.6 80.9 %forward0.1 = (f32[4096,2176]{1,0:T(8,128)}, f32[4096,2176]{1,0:T(8,128)}, bf16[4096,2176]{1,0:T(8,128)(2,1)}, bf16[2176,4096]{1,0:T(8,128)(2,1)}, bf16[640,4096...) custom-call(bf16[4096,640]{1,0:T(8,128)(2,1)} %bitcast.6, ...), custom_call_target="tpu_custom_call" | custom-call | flops 22817013760 | bytes 110000000 | tf_op jit(solution)/shard_map/forward0/pallas_call | solution.py:204
  81.5 100.0 %layer1.1 = (bf16[4096,640]{1,0:T(8,128)(2,1)}, bf16[640,4096]{1,0:T(8,128)(2,1)}, bf16[2176,4096]{1,0:T(8,128)(2,1)}, bf16[4096,4352]{1,0:T(8,128)(2,1)}) custom-call(bf16[4096,640]{1,0:T(8,128)(2,1)} %bitcast.7, bf16[4096,2176]{1,0:T(8,128)(2,1)} %get-tuple-element.19.act0_ref, bf16[4096,640]{1,0:T(8,128)(2,1)} %bitcast.9, ...), custom_call_target="tpu_custom_call" | custom-call | flops 68451041280 | bytes 100000000 | tf_op jit(solution)/shard_map/layer1/pallas_call | solution.py:262
  181.5 43.9 %backward0.1.dgu0_ref.tile_ref = bf16[4096,4352]{1,0:T(8,128)(2,1)} custom-call(bf16[4096,640]{1,0:T(8,128)(2,1)} %get-tuple-element.24.dh_ref.dht_ref.dh, f32[4096,2176]{1,0:T(8,128)} %get-tuple-element.25.gate_ref, f32[4096,2176]{1,0:T(8,128)} %get-tuple-element.26.up_ref, bf16[2,2176,640]{2,1,0:T(8,128)(2,1)} %get-tuple-element.22.wdn), custom_call_target="tpu_custom_call" | custom-call | flops 11408506880 | bytes 112000000 | tf_op jit(solution)/shard_map/backward0/pallas_call | solution.py:292
  225.4 163.4 %weights_and_input.1 = (bf16[4096,640]{1,0:T(8,128)(2,1)}, bf16[2,2,2,40,4352]{4,3,2,1,0:T(8,128)(2,1)}, bf16[2,544,640]{2,1,0:T(8,128)(2,1)}) custom-call(bf16[4096,4352]{1,0:T(8,128)(2,1)} %get-tuple-element.23.dgu1_ref, bf16[4096,4352]{1,0:T(8,128)(2,1)} %backward0.1.dgu0_ref.tile_ref, bf16[4096,640]{1,0:T(8,128)(2,1)} %bitcast.8, ...), custom_call_target="tpu_custom_call" | custom-call | flops 91268055040 | bytes 150000000 | tf_op jit(solution)/shard_map/weights_and_input/pallas_call | solution.py:494
  388.8 0.0 copy-start
  388.8 3.7 fusion
  392.5 0.3 copy-done
  392.8 0.0 copy-start.1
  392.8 2.4 copy.11
  395.2 0.0 copy-done.1
  395.2 1.1 copy.12
Async XLA Ops:
  388.8 4.0 %copy-start = (bf16[4096,640]{1,0:T(8,128)(2,1)S(1)}, bf16[4096,640]{1,0:T(8,128)(2,1)}, u32[]{:S(2)}) copy-start(bf16[4096,640]{1,0:T(8,128)(2,1)} %get-tuple-element.31) | copy-start | bytes 15728644
  392.8 2.4 copy-start.1
